TPU v7x, 256 devices: a whole 4x4x8 slice. The times are simulated.
256 devices in a mesh: dp: 8 (over z_lo, core), vocab: 32 (over z_hi, x, y).
Axes of the slice: x: 4, y: 4, z: 8 (z_hi: 2, z_lo: 4; z = z_hi * 4 + z_lo), core: 2. Of those that a mesh axis runs over, the one named last changes fastest.
Arguments:
- policy_hidden: bfloat16 [1024, 4096], P('dp'), may hold values from -84 to 84
- policy_weight: bfloat16 [4096, 65536], P('dp', 'vocab'), may hold values from -0.09375 to 0.09375
- reference_hidden: bfloat16 [1024, 4096], P(('dp', 'vocab')), may hold values from -84 to 84
- reference_weight: bfloat16 [4096, 65536], P(None, ('dp', 'vocab')), may hold values from -0.09375 to 0.09375
- targets: int32 [1024], replicated, may hold values from 0 to 65535
- response_mask: int32 [1024], replicated, may hold values 0 or 1
- pair_index: int32 [32], replicated, may hold values from 0 to 31, each once
Outputs:
- hidden_grad: bfloat16 [1024, 4096], P('vocab', 'dp')
- weight_grad: bfloat16 [4096, 65536], P('dp', 'vocab')
- total_loss: float32 [], replicated
Inputs may be any that keep to these rules, and one draw needn't show every extreme that they name: `pair_index`: each number of 0 to 31 once; entries 2p and 2p + 1 are the chosen and the rejected sequence of pair p.
All inputs are finite; a program needn't handle non-finite values.
Results may differ from a plain program's by a relative error of at most 0.005.
The roundings to bfloat16 on the way count: a program that leaves them out, or rounds other values in their place, can miss the bound.
Values may be sent and summed in bfloat16 or wider, within the bound.
A program may use at most 128 MiB of HBM per device.

v0:
```python
import jax
import jax.numpy as jnp
from jax import lax
from jax.sharding import Mesh
from jax.sharding import PartitionSpec as P

SEQ_LEN = 32
DP = ("dp_0", "dp_1")
VOCAB = ("vocab_0", "vocab_1", "vocab_2")
DP_VOCAB = ("dp_0", "dp_1", "vocab_0", "vocab_1", "vocab_2")
beta = 0.1
loss_scale = 4096.0


def all_in_one(value, axis):
    leaves = jax.tree.leaves(value)
    order = sorted(range(len(leaves)), key=lambda k: -leaves[k].size)
    width = (1, *leaves[order[0]].shape)[-1]
    lines = [
        jnp.pad(leaves[k].reshape(-1), (0, -leaves[k].size % width)).reshape(-1, width)
        for k in order
    ]
    both, at, found = (lax.all_gather(jnp.concatenate(lines), axis), 0, {})
    for k, line in zip(order, lines):
        slab = both[:, at : at + len(line)].reshape(len(both), -1)
        found[k] = slab[:, : leaves[k].size].reshape(-1, *leaves[k].shape)
        at += len(line)
    numbers = iter(range(len(leaves)))
    return jax.tree.map(lambda _: found[next(numbers)], value)


def merged_by_axis(value, axes, combine):
    for axis in axes:
        pieces = all_in_one(value, axis)
        value = jax.tree.map(lambda part: part[0], pieces)
        for k in range(1, lax.axis_size(axis)):
            value = combine(value, jax.tree.map(lambda part: part[k], pieces))
    return value


def in_blocks(value, dim, peers):
    shape = value.shape
    tiles = value.reshape(*shape[:dim], peers, shape[dim] // peers, *shape[dim + 1 :])
    return jnp.moveaxis(tiles, dim, 0)


def sum_at_owner(value, axis, dim):
    peers = lax.axis_size(axis)
    tiles = lax.all_to_all(in_blocks(value, dim, peers), axis, 0, 0, tiled=True)
    return jnp.sum(tiles, axis=0)


def pair_terms(log_ratio, pair_index):
    chosen = pair_index[0::2]
    rejected = pair_index[1::2]
    margin = beta * (log_ratio[chosen] - log_ratio[rejected])
    pair_count = chosen.shape[0]
    total_loss = jnp.sum(jax.nn.softplus(-margin)) / pair_count
    weight = -beta * loss_scale * jax.nn.sigmoid(-margin) / pair_count
    numbers = jnp.arange(log_ratio.shape[0], dtype=jnp.int32)[:, None]
    factor = jnp.sum(
        jnp.where(numbers == chosen[None, :], weight[None, :], 0.0)
        - jnp.where(numbers == rejected[None, :], weight[None, :], 0.0),
        axis=1,
    )
    return (total_loss, factor)


def local_pick(logits, targets, offset, axis):
    column_ids = lax.broadcasted_iota(jnp.int32, logits.shape, axis)
    shifted = targets - offset
    wanted = shifted[:, None] if axis == 1 else shifted[None, :]
    return jnp.sum(jnp.where(column_ids == wanted, logits, 0.0), axis=axis)


def merge_pair(earlier, later):
    largest = jnp.maximum(earlier[0], later[0])
    exp_total = earlier[1] * jnp.exp(earlier[0] - largest) + later[1] * jnp.exp(later[0] - largest)
    return (largest, exp_total, earlier[2] + later[2])


def merge_heads(earlier, later):
    return merge_pair(earlier[0:3], later[0:3]) + merge_pair(earlier[3:6], later[3:6])


def local(
    policy_hidden,
    policy_weight,
    reference_hidden,
    reference_weight,
    targets,
    response_mask,
    pair_index,
):
    data_index = lax.axis_index(DP)
    vocab_index = lax.axis_index(VOCAB)
    vocab_devices = lax.axis_size(VOCAB)
    data_devices = lax.axis_size(DP)
    policy_width = policy_weight.shape[1]
    reference_width = reference_weight.shape[1]
    active = response_mask.astype(jnp.float32)
    columns = lax.all_to_all(policy_hidden, DP, split_axis=1, concat_axis=0, tiled=True)
    reference_rows = reference_hidden
    for axis in ("dp_0", "vocab_0", "vocab_2", "vocab_1", "dp_1"):
        reference_rows = lax.all_gather(reference_rows, axis, axis=0, tiled=True)
    reference_logits = jnp.dot(reference_rows, reference_weight, preferred_element_type=jnp.float32)
    reference_targets = targets.reshape(4, 2, 2, 4, 4, 4).transpose(1, 3, 4, 2, 0, 5).reshape(-1)

    def in_order(value):
        return value.reshape(2, 4, 4, 2, 4, 4).transpose(4, 0, 3, 1, 2, 5).reshape(-1)

    reference_offset = (data_index * vocab_devices + vocab_index) * reference_width
    reference_top = jnp.max(reference_logits, axis=1)
    reference_pick = local_pick(reference_logits, reference_targets, reference_offset, 1)
    slice_width = policy_width // data_devices
    weight_block = policy_weight
    policy_logits = lax.psum_scatter(
        lax.dot_general(
            weight_block, columns, (((0,), (1,)), ((), ())), preferred_element_type=jnp.float32
        ),
        DP,
        scatter_dimension=0,
        tiled=True,
    )
    policy_offset = vocab_index * policy_width + data_index * slice_width
    policy_top = jnp.max(policy_logits, axis=0)
    policy_pick = local_pick(policy_logits, targets, policy_offset, 0)
    local_stats = (
        policy_top,
        jnp.sum(jnp.exp(policy_logits - policy_top[None, :]), axis=0),
        policy_pick,
        in_order(reference_top),
        in_order(jnp.sum(jnp.exp(reference_logits - reference_top[:, None]), axis=1)),
        in_order(reference_pick),
    )
    merged = merged_by_axis(local_stats, DP_VOCAB, merge_heads)
    policy_total = merged[0] + jnp.log(merged[1])
    reference_logp = merged[5] - merged[3] - jnp.log(merged[4])
    log_ratio = jnp.sum(
        (active * (merged[2] - policy_total - reference_logp)).reshape(-1, SEQ_LEN), axis=1
    )
    total_loss, factor = pair_terms(log_ratio, pair_index)
    token_scale = active * jnp.repeat(factor, SEQ_LEN)
    row_ids = lax.broadcasted_iota(jnp.int32, policy_logits.shape, 0)
    onehot = (row_ids == (targets - policy_offset)[None, :]).astype(jnp.float32)
    logit_grad = (
        token_scale[None, :] * (onehot - jnp.exp(policy_logits - policy_total[None, :]))
    ).astype(jnp.bfloat16)
    segment = lax.all_gather(logit_grad, DP, axis=0, tiled=True)
    weight_block = policy_weight
    column_grad = lax.dot_general(
        columns, segment, (((0,), (1,)), ((), ())), preferred_element_type=jnp.float32
    )
    hidden_part = lax.dot_general(
        segment, weight_block, (((0,), (1,)), ((), ())), preferred_element_type=jnp.float32
    )
    weight_grad, hidden_part = (column_grad, hidden_part)
    hidden_grad = sum_at_owner(hidden_part, VOCAB, 0)
    return (hidden_grad.astype(jnp.bfloat16), weight_grad.astype(jnp.bfloat16), total_loss)


def solution(mesh):
    torus = Mesh(
        mesh.devices.reshape(4, 2, 2, 4, 4), ("dp_0", "dp_1", "vocab_0", "vocab_1", "vocab_2")
    )
    in_specs = (P(DP, None), P(DP, VOCAB), P(DP_VOCAB, None), P(None, DP_VOCAB), P(), P(), P())
    out_specs = (P(VOCAB, DP), P(DP, VOCAB), P())
    return jax.shard_map(local, mesh=torus, in_specs=in_specs, out_specs=out_specs, check_vma=False)
```

profile of v0, /device:TPU:38, one launch (start us, length us, event | category | flops | bytes accessed | tf_op | source)
XLA Modules:
  0.0 438.4 jit_solution(6761728711644219476)
XLA Ops:
  8.1 14.9 %all-gather.5 = bf16[4,4,4096]{2,1,0:T(4,128)(2,1)S(1)} all-gather(bf16[1,4,4096]{2,1,0:T(4,128)(2,1)} %bitcast.468), channel_id=1, replica_groups=mesh['dp_0'=4,'dp_1'=2,'vocab_0'=2,'vocab_1'=4,'vocab_2'=4] {'dp_0'}, dimensions={0}, use_global_device_ids=true | all-gather | bytes 163840 | tf_op jit(solution)/shard_map/all_gather | solution.py:105
  23.0 9.7 %all_gather.49 = bf16[32,4096]{1,0:T(8,128)(2,1)} all-gather(bf16[16,4096]{1,0:T(8,128)(2,1)S(1)} %reshape.1628), channel_id=1, replica_groups=mesh['dp_0'=4,'dp_1'=2,'vocab_0'=2,'vocab_1'=4,'vocab_2'=4] {'vocab_0'}, dimensions={0}, use_global_device_ids=true | all-gather | bytes 393216 | tf_op jit(solution)/shard_map/all_gather | solution.py:105
  32.8 28.1 %all-gather.16.cloned.1.call-done = bf16[128,4096]{1,0:T(8,128)(2,1)} async-done(((bf16[32,4096]{1,0:T(8,128)(2,1)}), bf16[128,4096]{1,0:T(8,128)(2,1)}) %all-gather.16.cloned.1.call-update) | async-done | bytes 1048592 | tf_op jit(solution)/shard_map/all_gather | solution.py:105
  61.0 51.3 %all-gather.18.cloned.1.call-done = bf16[512,4096]{1,0:T(8,128)(2,1)} async-done(((bf16[128,4096]{1,0:T(8,128)(2,1)}), bf16[512,4096]{1,0:T(8,128)(2,1)}) %all-gather.18.cloned.1.call-update) | async-done | bytes 4194320 | tf_op jit(solution)/shard_map/all_gather | solution.py:105
  112.3 1.1 copy-done.2
  113.5 1.3 copy.26
  114.8 29.5 %all_to_all.24 = bf16[128,8,512]{0,2,1:T(8,128)(2,1)S(1)} all-to-all(bf16[128,8,512]{0,2,1:T(8,128)(2,1)} %bitcast.454), channel_id=1, replica_groups=mesh['dp_0'=4,'dp_1'=2,'vocab_0'=2,'vocab_1'=4,'vocab_2'=4] {'dp_0','dp_1'}, dimensions={1} | all-to-all | bytes 2097152 | tf_op jit(solution)/shard_map/all_to_all | solution.py:102
  144.3 1.3 copy.27
  145.6 6.8 %fusion.94 = f32[2048,1024]{1,0:T(8,128)} fusion(bf16[512,2048]{1,0:T(8,128)(2,1)S(1)} %copy-done, bf16[1024,512]{1,0:T(8,128)(2,1)} %bitcast.456), kind=kOutput, calls=%fused_computation.187 | convolution fusion | flops 2147483648 | bytes 11534336 | tf_op jit(solution)/shard_map/dot_general | solution.py:118
  152.6 0.6 copy-done.6
  153.1 0.1 slice.613
  153.2 0.1 slice.516
  153.4 0.2 sub.464
  153.6 0.1 copy.30
  153.7 0.2 sub.466
  153.9 6.4 %fusion.93 = (f32[1024]{0:T(1024)S(1)}, f32[1024,256]{0,1:T(8,128)S(1)}) fusion(bf16[1024,4096]{1,0:T(8,128)(2,1)} %all-gather.20.cloned.1.call-done, bf16[4096,256]{1,0:T(8,128)(2,1)} %param.10), kind=kOutput, calls=%fused_computation.186 | convolution fusion | flops 2147744768 | bytes 11538432 | tf_op jit(solution)/shard_map/dot_general | solution.py:106
  160.3 0.2 reshape.1595
  160.5 0.3 select_reduce_fusion
  160.7 0.2 reshape.1599
  161.0 0.2 reshape.1600
  161.2 0.2 reshape.1596
  161.3 0.2 reshape.1597
  161.6 0.2 reshape.1598
  161.8 84.9 %reduce-scatter.2.cloned.1.call-done = f32[256,1024]{1,0:T(8,128)} async-done(((f32[2048,1024]{1,0:T(8,128)}), f32[256,1024]{1,0:T(8,128)}) %reduce-scatter.2.cloned.1.call-update) | async-done | bytes 1048592 | tf_op jit(solution)/shard_map/reduce_scatter | solution.py:117
  246.6 1.3 reduce_max.18
  248.0 1.6 select_reduce_fusion.1
  249.6 14.0 %all-gather.6 = f32[4,6,1024]{2,1,0:T(8,128)S(1)} all-gather(f32[1,6,1024]{2,1,0:T(8,128)S(1)} %bitcast.462), channel_id=2, replica_groups=mesh['dp_0'=4,'dp_1'=2,'vocab_0'=2,'vocab_1'=4,'vocab_2'=4] {'dp_0'}, dimensions={0}, use_global_device_ids=true | all-gather | bytes 122880 | tf_op jit(solution)/shard_map/all_gather | solution.py:23
  263.7 0.1 fusion.39
  263.8 1.9 all-gather.7
  265.8 8.5 %all-gather.8 = f32[2,6,1024]{2,1,0:T(8,128)S(1)} all-gather(f32[1,6,1024]{2,1,0:T(8,128)S(1)} %bitcast.464), channel_id=4, replica_groups=mesh['dp_0'=4,'dp_1'=2,'vocab_0'=2,'vocab_1'=4,'vocab_2'=4] {'vocab_0'}, dimensions={0}, use_global_device_ids=true | all-gather | bytes 73728 | tf_op jit(solution)/shard_map/all_gather | solution.py:23
  274.4 12.0 %all-gather.9 = f32[4,6,1024]{2,1,0:T(8,128)S(1)} all-gather(f32[1,6,1024]{2,1,0:T(8,128)S(1)} %bitcast.465), channel_id=5, replica_groups=mesh['dp_0'=4,'dp_1'=2,'vocab_0'=2,'vocab_1'=4,'vocab_2'=4] {'vocab_1'}, dimensions={0}, use_global_device_ids=true | all-gather | bytes 122880 | tf_op jit(solution)/shard_map/all_gather | solution.py:23
  286.4 0.1 fusion.3
  286.6 12.6 %all-gather.10 = f32[4,6,1024]{2,1,0:T(8,128)S(1)} all-gather(f32[1,6,1024]{2,1,0:T(8,128)S(1)} %bitcast.466), channel_id=6, replica_groups=mesh['dp_0'=4,'dp_1'=2,'vocab_0'=2,'vocab_1'=4,'vocab_2'=4] {'vocab_2'}, dimensions={0}, use_global_device_ids=true | all-gather | bytes 122880 | tf_op jit(solution)/shard_map/all_gather | solution.py:23
  299.4 0.1 reduce_sum.76
  299.5 0.7 gather_fusion.1
  300.2 0.7 gather_fusion
  300.8 0.6 fusion.83
  301.5 0.1 subtract_reduce_fusion
  301.6 0.1 broadcast_in_dim.51
  301.6 0.1 reshape.1602
  301.7 1.1 multiply_convert_fusion
  302.8 51.4 %all-gather.22.cloned.1.call-done = bf16[2048,1024]{1,0:T(8,128)(2,1)} async-done(((bf16[256,1024]{1,0:T(8,128)(2,1)}), bf16[2048,1024]{1,0:T(8,128)(2,1)}) %all-gather.22.cloned.1.call-update) | async-done | bytes 4194320 | tf_op jit(solution)/shard_map/all_gather | solution.py:149
  354.2 5.9 %fusion.95 = f32[1024,512]{1,0:T(8,128)} fusion(bf16[2048,1024]{1,0:T(8,128)(2,1)} %all-gather.22.cloned.1.call-done, bf16[512,2048]{1,0:T(8,128)(2,1)S(1)} %copy-done), kind=kOutput, calls=%fused_computation.188 | convolution fusion | flops 2147483648 | bytes 8388608 | tf_op jit(solution)/shard_map/dot_general | solution.py:154
  360.1 13.1 %all-to-all-start.1 = ((f32[32,32,512]{2,1,0:T(8,128)}), f32[32,32,512]{2,1,0:T(8,128)}, u32[]{:S(2)}, u32[]{:S(2)}) async-start(f32[32,32,512]{2,1,0:T(8,128)} %bitcast.455), calls=%async_computation.2 | async-start | bytes 4194304 | tf_op jit(solution)/shard_map/all_to_all | solution.py:49
  373.9 5.9 %fusion = bf16[512,2048]{0,1:T(8,128)(2,1)} fusion(bf16[2048,1024]{1,0:T(8,128)(2,1)} %all-gather.22.cloned.1.call-done, bf16[1024,512]{1,0:T(8,128)(2,1)S(1)} %bitcast.457), kind=kOutput, calls=%fused_computation.3 | convolution fusion | flops 2148532224 | bytes 7340032 | tf_op jit(solution)/shard_map/dot_general | solution.py:151
  379.8 3.9 copy.32
  383.7 44.1 %all-to-all-done.1 = f32[32,32,512]{2,1,0:T(8,128)} async-done(((f32[32,32,512]{2,1,0:T(8,128)}), f32[32,32,512]{2,1,0:T(8,128)}, u32[]{:S(2)}, u32[]{:S(2)}) %all-to-all-start.1) | async-done | bytes 2097184 | tf_op jit(solution)/shard_map/all_to_all | solution.py:49
  427.8 2.4 reduce_sum.78
  (48 shorter events, 1.1 us)
Async XLA Ops:
  8.0 137.6 %copy-start = (bf16[512,2048]{1,0:T(8,128)(2,1)S(1)}, bf16[512,2048]{1,0:T(8,128)(2,1)}, u32[]{:S(2)}) copy-start(bf16[512,2048]{1,0:T(8,128)(2,1)} %param.8) | copy-start | bytes 6291460
  8.0 52.9 %all-gather.16.cloned.1.call-start = ((), (), s32[]{:S(2)}) async-start(), calls=%async_computation.4 | async-start | bytes 1310720 | tf_op jit(solution)/shard_map/all_gather | solution.py:105
  32.8 79.5 %all-gather.18.cloned.1.call-start = ((), (), s32[]{:S(2)}) async-start(), calls=%async_computation.5 | async-start | bytes 5242880 | tf_op jit(solution)/shard_map/all_gather | solution.py:105
  60.9 93.0 %all-gather.20.cloned.1.call-start = ((), (), s32[]{:S(2)}) async-start(), calls=%async_computation.6 | async-start | bytes 12582912 | tf_op jit(solution)/shard_map/all_gather | solution.py:105
  112.3 1.2 copy-start.2
  112.3 134.4 %reduce-scatter.2.cloned.1.call-start = ((), (), s32[]{:S(2)}) async-start(), calls=%async_computation.3 | async-start | bytes 9437184 | tf_op jit(solution)/shard_map/reduce_scatter | solution.py:117
  152.5 0.7 copy-start.6
  152.5 0.9 copy-start.5
  152.5 201.7 %all-gather.22.cloned.1.call-start = ((), (), s32[]{:S(2)}) async-start(), calls=%async_computation.7 | async-start | bytes 4718592 | tf_op jit(solution)/shard_map/all_gather | solution.py:149
  161.5 137.7 %copy-start.4 = (s32[1024]{0:T(1024)S(1)}, s32[1024]{0:T(1024)}, u32[]{:S(2)}) copy-start(s32[1024]{0:T(1024)} %param.12) | copy-start | bytes 12292
  247.9 53.8 %copy-start.1 = (f32[256,1024]{1,0:T(8,128)S(1)}, f32[256,1024]{1,0:T(8,128)}, u32[]{:S(2)}) copy-start(f32[256,1024]{1,0:T(8,128)} %reduce-scatter.2.cloned.1.call-done) | copy-start | bytes 3145732
  360.1 13.8 %copy-start.3 = (bf16[8,128,512]{2,1,0:T(8,128)(2,1)S(1)}, bf16[8,128,512]{2,1,0:T(8,128)(2,1)}, u32[]{:S(2)}) copy-start(bf16[8,128,512]{2,1,0:T(8,128)(2,1)} %copy.27) | copy-start | bytes 3145732
  360.1 67.7 %all-to-all-start.1 = ((f32[32,32,512]{2,1,0:T(8,128)}), f32[32,32,512]{2,1,0:T(8,128)}, u32[]{:S(2)}, u32[]{:S(2)}) async-start(f32[32,32,512]{2,1,0:T(8,128)} %bitcast.455), calls=%async_computation.2 | async-start | bytes 4194304 | tf_op jit(solution)/shard_map/all_to_all | solution.py:49
Sparse Core Ops, SparseCore 0:
  32.9 27.9 all-gather.15
  62.7 49.5 all-gather.17
  114.1 27.0 all-gather.19
Sparse Core Ops, SparseCore 1:
  152.6 94.0 reduce-scatter.1
  302.9 51.2 all-gather.21
where the time goes:
time: 439 us; the launch traced here: 438 us
  waiting for transfers between devices  260 us (59%)
  blocking collectives  103 us (23%)
  matrix products  25 us (6%)
  between operations  17.2 us (4%)
  starting transfers between devices  13.3 us (3%)
  local copies, waits for them, and re-layouts  11.9 us (3%)
  other arithmetic  7.93 us (2%)
    reduce_scatter x1, waiting for transfers between devices, local(): lax.psum_scatter(lax.dot_general(weight_block, columns, (((0,), (1,)), ((...  84.9 us
    all_gather x3, waiting for transfers between devices, local(): reference_rows = lax.all_gather(reference_rows, axis, axis=0, tiled=True)  79.4 us
    all_gather x1, waiting for transfers between devices, local(): segment = lax.all_gather(logit_grad, DP, axis=0, tiled=True)  51.4 us
    all_gather x5, blocking collectives, all_in_one(): both, at, found = (lax.all_gather(jnp.concatenate(lines), axis), 0, {})  49 us
    all_to_all x1, waiting for transfers between devices, sum_at_owner(): tiles = lax.all_to_all(in_blocks(value, dim, peers), axis, 0, 0, tiled=True)  44.1 us
    all_to_all x1, blocking collectives, local(): lax.all_to_all(policy_hidden, DP, split_axis=1, concat_axis=0, tiled=True)  29.5 us
    all_gather x2, blocking collectives, local(): reference_rows = lax.all_gather(reference_rows, axis, axis=0, tiled=True)  24.6 us
    all_to_all x1, starting transfers between devices, sum_at_owner(): tiles = lax.all_to_all(in_blocks(value, dim, peers), axis, 0, 0, tiled=True)  13.1 us
  transfers between devices with their start and end apart: 6, of which 5 were waited for; matrix products, arithmetic and copies ran while one was open for 6% of the time, Pallas kernels for 0%

commit v1 on v0

--- a/solution.py
+++ b/solution.py
@@ -102,7 +102,9 @@
     columns = lax.all_to_all(policy_hidden, DP, split_axis=1, concat_axis=0, tiled=True)
     reference_rows = reference_hidden
     for axis in ("dp_0", "vocab_0", "vocab_2", "vocab_1", "dp_1"):
-        reference_rows = lax.all_gather(reference_rows, axis, axis=0, tiled=True)
+        reference_rows = jnp.concatenate(
+            lax.all_to_all(jnp.stack([reference_rows] * lax.axis_size(axis)), axis, 0, 0), axis=0
+        )
     reference_logits = jnp.dot(reference_rows, reference_weight, preferred_element_type=jnp.float32)
     reference_targets = targets.reshape(4, 2, 2, 4, 4, 4).transpose(1, 3, 4, 2, 0, 5).reshape(-1)
 

time: 439 us -> 360 us (0.82)
  waiting for transfers between devices: 260 us -> 136 us
  blocking collectives: 103 us -> 137 us
  other arithmetic: 7.93 us -> 15.4 us
  starting transfers between devices: 13.3 us -> 18.7 us
    reduce_scatter x1, waiting for transfers between devices: 84.9 us -> 0.01 us  [local(): lax.psum_scatter(lax.dot_general(weight_block, columns, (((0,), (1,)), ((...]
    all_gather x3 -> x0, waiting for transfers between devices: 79.4 us -> none  [local(): reference_rows = lax.all_gather(reference_rows, axis, axis=0, tiled=True)]
    all_to_all x0 -> x4, blocking collectives: none -> 60.1 us  [local(): lax.all_to_all(jnp.stack([reference_rows] * lax.axis_size(axis)), axis, 0...]
    all_to_all x0 -> x1, waiting for transfers between devices: none -> 43.1 us  [local(): lax.all_to_all(jnp.stack([reference_rows] * lax.axis_size(axis)), axis, 0...]
    all_gather x2 -> x0, blocking collectives: 24.6 us -> none  [local(): reference_rows = lax.all_gather(reference_rows, axis, axis=0, tiled=True)]
    another operation x0 -> x2, other arithmetic: none -> 7.47 us  [local(): jnp.stack([reference_rows] * lax.axis_size(axis))]
    all_to_all x0 -> x1, starting transfers between devices: none -> 5.39 us  [local(): lax.all_to_all(jnp.stack([reference_rows] * lax.axis_size(axis)), axis, 0...]
  transfers between devices with their start and end apart: 6 -> 4, of which waited for: 5 -> 3; matrix products, arithmetic and copies ran while one was open for 6% -> 7% of each run, Pallas kernels for 0% -> 0%
where the time goes in v1:
time: 360 us; the launch traced here: 359 us
  blocking collectives  137 us (38%)
  waiting for transfers between devices  136 us (38%)
  matrix products  21.1 us (6%)
  starting transfers between devices  18.7 us (5%)
  between operations  16.1 us (4%)
  other arithmetic  15.4 us (4%)
  local copies, waits for them, and re-layouts  14.6 us (4%)
    all_to_all x4, blocking collectives, local(): lax.all_to_all(jnp.stack([reference_rows] * lax.axis_size(axis)), axis, 0...  60.1 us
    all_gather x1, waiting for transfers between devices, local(): segment = lax.all_gather(logit_grad, DP, axis=0, tiled=True)  48.5 us
    all_gather x5, blocking collectives, all_in_one(): both, at, found = (lax.all_gather(jnp.concatenate(lines), axis), 0, {})  47 us
    all_to_all x1, waiting for transfers between devices, sum_at_owner(): tiles = lax.all_to_all(in_blocks(value, dim, peers), axis, 0, 0, tiled=True)  44.1 us
    all_to_all x1, waiting for transfers between devices, local(): lax.all_to_all(jnp.stack([reference_rows] * lax.axis_size(axis)), axis, 0...  43.1 us
    all_to_all x1, blocking collectives, local(): lax.all_to_all(policy_hidden, DP, split_axis=1, concat_axis=0, tiled=True)  30.3 us
    all_to_all x1, starting transfers between devices, sum_at_owner(): tiles = lax.all_to_all(in_blocks(value, dim, peers), axis, 0, 0, tiled=True)  13.2 us
    another operation x2, other arithmetic, local(): jnp.stack([reference_rows] * lax.axis_size(axis))  7.47 us
  transfers between devices with their start and end apart: 4, of which 3 were waited for; matrix products, arithmetic and copies ran while one was open for 7% of the time, Pallas kernels for 0%

profile of v1, /device:TPU:38, one launch (start us, length us, event | category | flops | bytes accessed | tf_op | source)
XLA Modules:
  0.0 359.0 jit_solution(1359510357651416290)
XLA Ops:
  7.2 2.4 copy.26
  9.6 30.3 %all_to_all.49 = bf16[128,8,512]{0,2,1:T(8,128)(2,1)S(1)} all-to-all(bf16[128,8,512]{0,2,1:T(8,128)(2,1)} %bitcast.459), channel_id=1, replica_groups=mesh['dp_0'=4,'dp_1'=2,'vocab_0'=2,'vocab_1'=4,'vocab_2'=4] {'dp_0','dp_1'}, dimensions={1} | all-to-all | bytes 2097152 | tf_op jit(solution)/shard_map/all_to_all | solution.py:102
  39.9 1.3 copy.27
  41.2 6.8 %fusion.94 = f32[2048,1024]{1,0:T(8,128)} fusion(bf16[512,2048]{1,0:T(8,128)(2,1)S(1)} %copy-done, bf16[1024,512]{1,0:T(8,128)(2,1)} %bitcast.462), kind=kOutput, calls=%fused_computation.189 | convolution fusion | flops 2147483648 | bytes 11534336 | tf_op jit(solution)/shard_map/dot_general | solution.py:120
  48.1 0.7 copy-done.3
  48.8 9.8 %all_to_all.50 = bf16[4,4,4096]{2,1,0:T(4,128)(2,1)S(1)} all-to-all(bf16[4,4,4096]{2,1,0:T(4,128)(2,1)S(1)} %stack.19), channel_id=1, replica_groups=mesh['dp_0'=4,'dp_1'=2,'vocab_0'=2,'vocab_1'=4,'vocab_2'=4] {'dp_0'}, dimensions={0} | all-to-all | bytes 262144 | tf_op jit(solution)/shard_map/all_to_all | solution.py:106
  58.8 20.9 %all_to_all.51 = bf16[2,16,4096]{2,1,0:T(8,128)(2,1)S(1)} all-to-all(bf16[2,16,4096]{2,1,0:T(8,128)(2,1)S(1)} %pad_maximum_fusion.1), channel_id=1, replica_groups=mesh['dp_0'=4,'dp_1'=2,'vocab_0'=2,'vocab_1'=4,'vocab_2'=4] {'vocab_0'}, dimensions={0} | all-to-all | bytes 524288 | tf_op jit(solution)/shard_map/all_to_all | solution.py:106
  79.6 0.1 stack.21
  79.8 17.2 %all_to_all.52 = bf16[4,32,4096]{2,1,0:T(8,128)(2,1)S(1)} all-to-all(bf16[4,32,4096]{2,1,0:T(8,128)(2,1)S(1)} %stack.21), channel_id=1, replica_groups=mesh['dp_0'=4,'dp_1'=2,'vocab_0'=2,'vocab_1'=4,'vocab_2'=4] {'vocab_2'}, dimensions={0} | all-to-all | bytes 2097152 | tf_op jit(solution)/shard_map/all_to_all | solution.py:106
  96.9 2.5 stack.22
  99.4 5.4 %all-to-all-start.4 = ((bf16[4,128,4096]{2,1,0:T(8,128)(2,1)}), bf16[4,128,4096]{2,1,0:T(8,128)(2,1)}, u32[]{:S(2)}, u32[]{:S(2)}) async-start(bf16[4,128,4096]{2,1,0:T(8,128)(2,1)} %stack.22), calls=%async_computation.5 | async-start | bytes 8388608 | tf_op jit(solution)/shard_map/all_to_all | solution.py:106
  104.8 0.1 slice.613
  104.9 0.1 slice.516
  105.1 0.2 sub.464
  105.3 0.2 sub.466
  105.5 43.1 %all-to-all-done.4 = bf16[4,128,4096]{2,1,0:T(8,128)(2,1)} async-done(((bf16[4,128,4096]{2,1,0:T(8,128)(2,1)}), bf16[4,128,4096]{2,1,0:T(8,128)(2,1)}, u32[]{:S(2)}, u32[]{:S(2)}) %all-to-all-start.4) | async-done | bytes 4194336 | tf_op jit(solution)/shard_map/all_to_all | solution.py:106
  148.6 7.4 %pad_maximum_fusion = bf16[2,512,4096]{2,1,0:T(8,128)(2,1)} fusion(bf16[1,512,4096]{2,1,0:T(8,128)(2,1)} %bitcast.8), kind=kLoop, calls=%fused_computation.2 | loop fusion | flops 4194304 | bytes 12582912 | tf_op jit(solution)/shard_map/stack | solution.py:106
  156.1 12.2 %all_to_all.53 = bf16[2,512,4096]{2,1,0:T(8,128)(2,1)S(1)} all-to-all(bf16[2,512,4096]{2,1,0:T(8,128)(2,1)} %pad_maximum_fusion), channel_id=1, replica_groups=mesh['dp_0'=4,'dp_1'=2,'vocab_0'=2,'vocab_1'=4,'vocab_2'=4] {'dp_1'}, dimensions={0} | all-to-all | bytes 16777216 | tf_op jit(solution)/shard_map/all_to_all | solution.py:106
  168.3 2.4 fusion.93
  170.7 0.2 reshape.1605
  170.9 0.3 select_reduce_fusion
  171.2 0.2 reshape.1609
  171.4 0.2 reshape.1610
  171.6 0.2 reshape.1606
  171.8 0.2 reshape.1607
  172.0 0.2 reshape.1608
  172.2 1.4 reduce_max.18
  173.6 1.5 select_reduce_fusion.1
  175.1 12.4 %all-gather.5 = f32[4,6,1024]{2,1,0:T(8,128)S(1)} all-gather(f32[1,6,1024]{2,1,0:T(8,128)S(1)} %bitcast.468), channel_id=2, replica_groups=mesh['dp_0'=4,'dp_1'=2,'vocab_0'=2,'vocab_1'=4,'vocab_2'=4] {'dp_0'}, dimensions={0}, use_global_device_ids=true | all-gather | bytes 122880 | tf_op jit(solution)/shard_map/all_gather | solution.py:23
  187.6 0.1 fusion.39
  187.7 1.9 all-gather.6
  189.7 8.5 %all-gather.7 = f32[2,6,1024]{2,1,0:T(8,128)S(1)} all-gather(f32[1,6,1024]{2,1,0:T(8,128)S(1)} %bitcast.470), channel_id=4, replica_groups=mesh['dp_0'=4,'dp_1'=2,'vocab_0'=2,'vocab_1'=4,'vocab_2'=4] {'vocab_0'}, dimensions={0}, use_global_device_ids=true | all-gather | bytes 73728 | tf_op jit(solution)/shard_map/all_gather | solution.py:23
  198.3 12.1 %all-gather.8 = f32[4,6,1024]{2,1,0:T(8,128)S(1)} all-gather(f32[1,6,1024]{2,1,0:T(8,128)S(1)} %bitcast.471), channel_id=5, replica_groups=mesh['dp_0'=4,'dp_1'=2,'vocab_0'=2,'vocab_1'=4,'vocab_2'=4] {'vocab_1'}, dimensions={0}, use_global_device_ids=true | all-gather | bytes 122880 | tf_op jit(solution)/shard_map/all_gather | solution.py:23
  210.4 0.1 fusion.3
  210.6 12.2 %all-gather.9 = f32[4,6,1024]{2,1,0:T(8,128)S(1)} all-gather(f32[1,6,1024]{2,1,0:T(8,128)S(1)} %bitcast.472), channel_id=6, replica_groups=mesh['dp_0'=4,'dp_1'=2,'vocab_0'=2,'vocab_1'=4,'vocab_2'=4] {'vocab_2'}, dimensions={0}, use_global_device_ids=true | all-gather | bytes 122880 | tf_op jit(solution)/shard_map/all_gather | solution.py:23
  223.0 0.1 reduce_sum.76
  223.1 0.7 gather_fusion.1
  223.8 0.7 gather_fusion
  224.4 0.6 fusion.83
  225.1 0.1 subtract_reduce_fusion
  225.3 1.1 multiply_convert_fusion
  226.4 48.5 %all-gather.12.cloned.1.call-done = bf16[2048,1024]{1,0:T(8,128)(2,1)} async-done(((bf16[256,1024]{1,0:T(8,128)(2,1)}), bf16[2048,1024]{1,0:T(8,128)(2,1)}) %all-gather.12.cloned.1.call-update) | async-done | bytes 4194320 | tf_op jit(solution)/shard_map/all_gather | solution.py:151
  275.0 5.9 %fusion.95 = f32[1024,512]{1,0:T(8,128)} fusion(bf16[2048,1024]{1,0:T(8,128)(2,1)} %all-gather.12.cloned.1.call-done, bf16[512,2048]{1,0:T(8,128)(2,1)S(1)} %copy-done), kind=kOutput, calls=%fused_computation.190 | convolution fusion | flops 2147483648 | bytes 8388608 | tf_op jit(solution)/shard_map/dot_general | solution.py:156
  280.9 13.2 %all-to-all-start.6 = ((f32[32,32,512]{2,1,0:T(8,128)}), f32[32,32,512]{2,1,0:T(8,128)}, u32[]{:S(2)}, u32[]{:S(2)}) async-start(f32[32,32,512]{2,1,0:T(8,128)} %bitcast.460), calls=%async_computation.7 | async-start | bytes 4194304 | tf_op jit(solution)/shard_map/all_to_all | solution.py:49
  294.8 5.9 %fusion = bf16[512,2048]{0,1:T(8,128)(2,1)} fusion(bf16[2048,1024]{1,0:T(8,128)(2,1)} %all-gather.12.cloned.1.call-done, bf16[1024,512]{1,0:T(8,128)(2,1)S(1)} %bitcast.463), kind=kOutput, calls=%fused_computation.4 | convolution fusion | flops 2148532224 | bytes 7340032 | tf_op jit(solution)/shard_map/dot_general | solution.py:153
  300.7 3.9 %copy.32 = bf16[512,2048]{1,0:T(8,128)(2,1)} copy(bf16[512,2048]{0,1:T(8,128)(2,1)} %fusion) | data formatting | bytes 4194304
  304.6 44.1 %all-to-all-done.6 = f32[32,32,512]{2,1,0:T(8,128)} async-done(((f32[32,32,512]{2,1,0:T(8,128)}), f32[32,32,512]{2,1,0:T(8,128)}, u32[]{:S(2)}, u32[]{:S(2)}) %all-to-all-start.6) | async-done | bytes 2097184 | tf_op jit(solution)/shard_map/all_to_all | solution.py:49
  348.7 2.4 reduce_sum.78
  (50 shorter events, 1.2 us)
Async XLA Ops:
  7.2 34.0 %copy-start = (bf16[512,2048]{1,0:T(8,128)(2,1)S(1)}, bf16[512,2048]{1,0:T(8,128)(2,1)}, u32[]{:S(2)}) copy-start(bf16[512,2048]{1,0:T(8,128)(2,1)} %param.8) | copy-start | bytes 6291460
  7.2 165.0 %reduce-scatter.2.cloned.1.call-start = ((), (), s32[]{:S(2)}) async-start(), calls=%async_computation.8 | async-start | bytes 9437184 | tf_op jit(solution)/shard_map/reduce_scatter | solution.py:119
  48.0 0.8 copy-start.3
  99.4 5.4 %copy-start.7 = (s32[32]{0:T(128)S(1)}, s32[32]{0:T(128)}, u32[]{:S(2)}) copy-start(s32[32]{0:T(128)} %param.13) | copy-start | bytes 388
  99.4 5.6 %copy-start.5 = (s32[1024]{0:T(1024)S(1)}, s32[1024]{0:T(1024)}, u32[]{:S(2)}) copy-start(s32[1024]{0:T(1024)} %param.11) | copy-start | bytes 12292
  99.4 49.2 %all-to-all-start.4 = ((bf16[4,128,4096]{2,1,0:T(8,128)(2,1)}), bf16[4,128,4096]{2,1,0:T(8,128)(2,1)}, u32[]{:S(2)}, u32[]{:S(2)}) async-start(bf16[4,128,4096]{2,1,0:T(8,128)(2,1)} %stack.22), calls=%async_computation.5 | async-start | bytes 8388608 | tf_op jit(solution)/shard_map/all_to_all | solution.py:106
  104.8 170.2 %all-gather.12.cloned.1.call-start = ((), (), s32[]{:S(2)}) async-start(), calls=%async_computation.9 | async-start | bytes 4718592 | tf_op jit(solution)/shard_map/all_gather | solution.py:151
  156.1 12.2 %copy-start.6 = (bf16[4096,256]{1,0:T(8,128)(2,1)S(1)}, bf16[4096,256]{1,0:T(8,128)(2,1)}, u32[]{:S(2)}) copy-start(bf16[4096,256]{1,0:T(8,128)(2,1)} %param.10) | copy-start | bytes 6291460
  170.7 52.2 %copy-start.4 = (s32[1024]{0:T(1024)S(1)}, s32[1024]{0:T(1024)}, u32[]{:S(2)}) copy-start(s32[1024]{0:T(1024)} %param.12) | copy-start | bytes 12292
  172.2 53.1 %copy-start.1 = (f32[256,1024]{1,0:T(8,128)S(1)}, f32[256,1024]{1,0:T(8,128)}, u32[]{:S(2)}) copy-start(f32[256,1024]{1,0:T(8,128)} %reduce-scatter.2.cloned.1.call-done) | copy-start | bytes 3145732
  280.9 13.9 %copy-start.2 = (bf16[8,128,512]{2,1,0:T(8,128)(2,1)S(1)}, bf16[8,128,512]{2,1,0:T(8,128)(2,1)}, u32[]{:S(2)}) copy-start(bf16[8,128,512]{2,1,0:T(8,128)(2,1)} %copy.27) | copy-start | bytes 3145732
  280.9 67.8 %all-to-all-start.6 = ((f32[32,32,512]{2,1,0:T(8,128)}), f32[32,32,512]{2,1,0:T(8,128)}, u32[]{:S(2)}, u32[]{:S(2)}) async-start(f32[32,32,512]{2,1,0:T(8,128)} %bitcast.460), calls=%async_computation.7 | async-start | bytes 4194304 | tf_op jit(solution)/shard_map/all_to_all | solution.py:49
Sparse Core Ops, SparseCore 0:
  48.2 99.6 reduce-scatter.1
  226.5 48.3 all-gather.11
